TPU v7x, 128 devices: a whole 4x4x4 slice. The times are simulated.
128 devices in a mesh: dp: 16 (over y, x_lo, core), shard: 8 (over z, x_hi).
Axes of the slice: x: 4 (x_hi: 2, x_lo: 2; x = x_hi * 2 + x_lo), y: 4, z: 4, core: 2. Of those that a mesh axis runs over, the one named last changes fastest.
Arguments:
- gradients: bfloat16 [16, 88, 512, 512], P('dp', 'shard'), may hold values from -60 to 60
- owners: int32 [8, 11], P('shard'), may hold values from 0 to 15, as said below
- block_param: int32 [88], replicated, may hold values from 0 to 6, never falling along the last dimension, each value on 1 to 25 neighbouring positions
- left_stat: float32 [32, 8, 512, 512], P('dp', 'shard'), may hold values from -4 to 8, as said below
- right_stat: float32 [32, 8, 512, 512], P('dp', 'shard'), may hold values from -4 to 8, as said below
- moment: float32 [32, 8, 512, 512], P('dp', 'shard'), may hold values from 0.5 to 50
- left_root: bfloat16 [32, 8, 512, 512], P('dp', 'shard'), may hold values from -1 to 3.5, as said below
- right_root: bfloat16 [32, 8, 512, 512], P('dp', 'shard'), may hold values from -1 to 3.5, as said below
Outputs:
- new_left: float32 [32, 8, 512, 512], P('dp', 'shard')
- new_right: float32 [32, 8, 512, 512], P('dp', 'shard')
- new_moment: float32 [32, 8, 512, 512], P('dp', 'shard')
- update: bfloat16 [88, 512, 512], P('shard')
Inputs may be any that keep to these rules, and one draw needn't show every extreme that they name: `owners`: in each row, no value occurs more than 2 times, and some value occurs exactly 2 times. `left_stat`: each slot's matrix is symmetric. `right_stat`: each slot's matrix is symmetric. `left_root`: each slot's matrix is symmetric. `right_root`: each slot's matrix is symmetric.
All inputs are finite; a program needn't handle non-finite values.
Results may differ from a plain program's by a relative error of at most 0.0058.
Values may be sent and summed in bfloat16 or wider, within the bound.
A program may use at most 192 MiB of HBM per device.

v0:
```python
import jax
import jax.numpy as jnp
from jax import lax
from jax.sharding import Mesh
from jax.sharding import PartitionSpec as P

NPARAM = 7
DP = ("dp_0", "dp_1", "dp_2")
SHARD = ("shard_0", "shard_1")
DP_SHARD = ("dp_0", "dp_1", "dp_2", "shard_0", "shard_1")
decay_rate = 0.95
tiny_value = 1e-06


def by_axis(x, axes):
    for axis in axes:
        x = lax.psum(x, axis)
    return x


def on_device(gradients, owners, block_param, left_stat, right_stat, moment, left_root, right_root):
    replicas = lax.axis_size(DP)
    capacity = left_stat.shape[0]
    blocks = gradients.shape[1]
    block_width = gradients.shape[3]
    device = lax.axis_index(DP)
    column = lax.axis_index(SHARD)
    owner_row = owners[0]
    counter = jnp.arange(blocks, dtype=jnp.int32)
    same_owner = owner_row[:, None] == owner_row[None, :]
    earlier = counter[None, :] < counter[:, None]
    places = owner_row * capacity + jnp.sum(jnp.where(same_owner & earlier, 1, 0), axis=1).astype(
        jnp.int32
    )
    slot_ids = jnp.arange(replicas * capacity, dtype=jnp.int32)
    matches = places[None, :] == slot_ids[:, None]
    source = jnp.min(jnp.where(matches, counter[None, :], blocks), axis=1)
    partials = gradients[0].astype(jnp.float32)
    row_share = lax.psum_scatter(partials, DP, scatter_dimension=1, tiled=True)
    share_padded = jnp.concatenate(
        [row_share, jnp.zeros((1,) + row_share.shape[1:], jnp.float32)], axis=0
    )
    outgoing = jnp.take(share_padded, source, axis=0).reshape(
        replicas, capacity, block_width // replicas, block_width
    )
    arrived = lax.all_to_all(outgoing, DP, split_axis=0, concat_axis=2, tiled=True)
    summed = arrived[0]
    left_gram = jnp.einsum("cij,ckj->cik", summed, summed, precision=lax.Precision.HIGHEST)
    right_gram = jnp.einsum("cji,cjk->cik", summed, summed, precision=lax.Precision.HIGHEST)
    new_left = decay_rate * left_stat + (1.0 - decay_rate) * left_gram[:, None]
    new_right = decay_rate * right_stat + (1.0 - decay_rate) * right_gram[:, None]
    new_moment = decay_rate * moment + (1.0 - decay_rate) * (summed * summed)[:, None]
    adam_step = summed / (jnp.sqrt(new_moment[:, 0]) + tiny_value)
    left_half = jnp.einsum(
        "cij,cjk->cik",
        left_root[:, 0],
        summed.astype(jnp.bfloat16),
        preferred_element_type=jnp.float32,
    ).astype(jnp.bfloat16)
    direction = jnp.einsum(
        "cij,cjk->cik", left_half, right_root[:, 0], preferred_element_type=jnp.float32
    )
    my_slots = lax.dynamic_slice_in_dim(matches, device * capacity, capacity, 0)
    local_params = lax.dynamic_slice_in_dim(block_param, column * blocks, blocks, 0)
    slot_param = jnp.sum(jnp.where(my_slots, local_params[None, :], 0), axis=1)
    is_live = jnp.any(my_slots, axis=1)
    param_ids = jnp.arange(NPARAM, dtype=jnp.int32)
    member = (slot_param[:, None] == param_ids[None, :]) & is_live[:, None]
    adam_squares = jnp.sum(adam_step * adam_step, axis=(1, 2))
    direction_squares = jnp.sum(direction * direction, axis=(1, 2))
    adam_local = jnp.sum(jnp.where(member, adam_squares[:, None], 0.0), axis=0)
    direction_local = jnp.sum(jnp.where(member, direction_squares[:, None], 0.0), axis=0)
    adam_norm, direction_norm = (by_axis(adam_local, DP_SHARD), by_axis(direction_local, DP_SHARD))
    graft_ratio = jnp.sqrt((adam_norm + tiny_value) / (direction_norm + tiny_value))
    slot_ratio = jnp.sum(jnp.where(member, graft_ratio[None, :], 0.0), axis=1)
    slot_update = (slot_ratio[:, None, None] * direction).astype(jnp.bfloat16)
    returned = lax.all_to_all(slot_update, DP, split_axis=1, concat_axis=0, tiled=True)
    pieces = jnp.take(returned, places, axis=0)
    update = lax.all_gather(pieces, DP, axis=1, tiled=True)
    return (new_left, new_right, new_moment, update)


def solution(mesh):
    finer = Mesh(
        mesh.devices.reshape(4, 2, 2, 4, 2), ("dp_0", "dp_1", "dp_2", "shard_0", "shard_1")
    )
    placed = (
        P(DP, SHARD, None, None),
        P(SHARD, None),
        P(),
        P(DP, SHARD, None, None),
        P(DP, SHARD, None, None),
        P(DP, SHARD, None, None),
        P(DP, SHARD, None, None),
        P(DP, SHARD, None, None),
    )
    return jax.shard_map(
        on_device,
        mesh=finer,
        in_specs=placed,
        out_specs=(
            P(DP, SHARD, None, None),
            P(DP, SHARD, None, None),
            P(DP, SHARD, None, None),
            P(SHARD, None, None),
        ),
        check_vma=False,
    )
```

profile of v0, /device:TPU:1, one launch (start us, length us, event | category | flops | bytes accessed | tf_op | source)
XLA Modules:
  0.0 309.6 jit_solution(17516869295652060086)
XLA Ops:
  7.2 0.0 copy-start
  7.2 0.0 reduce-scatter.2.cloned.1.call-start
  7.2 8.7 %bitcast_convert_fusion = f32[11,512,512]{2,1,0:T(8,128)} fusion(bf16[1,11,512,512]{3,2,1,0:T(8,128)(2,1)} %param.8), kind=kLoop, calls=%fused_computation.2 | loop fusion | flops 2883584 | bytes 17301504 | tf_op jit(solution)/shard_map/convert_element_type | solution.py:38
  15.9 0.0 reduce-scatter.2.cloned.1.call-update
  15.9 0.6 copy-done.6
  16.6 0.2 select_reduce_fusion.1
  16.7 0.1 select_reduce_fusion
  16.9 0.1 reduce_min.14
  17.0 130.2 %reduce-scatter.2.cloned.1.call-done = f32[11,32,512]{2,1,0:T(8,128)} async-done(((f32[11,512,512]{2,1,0:T(8,128)}), f32[11,32,512]{2,1,0:T(8,128)}) %reduce-scatter.2.cloned.1.call-update) | async-done | bytes 720912 | tf_op jit(solution)/shard_map/reduce_scatter | solution.py:39
  147.2 1.2 concatenate.3
  148.4 2.0 gather_fusion
  150.4 3.1 %broadcast_select_fusion = f32[16,2,32,512]{3,2,1,0:T(8,128)} fusion(f32[16,2,32,512]{3,2,1,0:T(8,128)} %bitcast.83, pred[16,2]{1,0:T(8,128)(4,1)S(1)} %compare_and_fusion), kind=kLoop, calls=%fused_computation.23 | loop fusion | flops 524288 | bytes 4194336 | tf_op jit(solution)/shard_map/jit(_take)/select_n | solution.py:43
  153.5 5.9 %all-to-all-start = ((f32[16,2,32,512]{3,2,1,0:T(8,128)}), f32[16,2,32,512]{3,2,1,0:T(8,128)S(1)}, u32[]{:S(2)}, u32[]{:S(2)}) async-start(f32[16,2,32,512]{3,2,1,0:T(8,128)} %broadcast_select_fusion), calls=%async_computation.1 | async-start | bytes 4194304 | tf_op jit(solution)/shard_map/all_to_all | solution.py:46
  159.3 0.1 dynamic_slice.7
  159.4 0.1 fusion.15
  159.5 0.1 select_reduce_fusion.5
  159.7 26.7 %all-to-all-done = f32[16,2,32,512]{3,2,1,0:T(8,128)S(1)} async-done(((f32[16,2,32,512]{3,2,1,0:T(8,128)}), f32[16,2,32,512]{3,2,1,0:T(8,128)S(1)}, u32[]{:S(2)}, u32[]{:S(2)}) %all-to-all-start) | async-done | bytes 2097184 | tf_op jit(solution)/shard_map/all_to_all | solution.py:46
  186.4 0.3 multiply_multiply_fusion
  186.6 1.1 copy-done.2
  187.7 0.2 copy.65
  187.9 0.0 copy-start.3
  188.0 2.0 copy.61
  189.9 0.3 copy-done.3
  190.2 2.8 sqrt_add_fusion
  193.0 4.0 %multiply_reduce_fusion = (f32[2]{0:T(128)S(1)}, f32[2,512,512]{2,1,0:T(8,128)}) fusion(bf16[2,1,512,512]{3,2,1,0:T(8,128)(2,1)S(1)} %copy-done, bf16[2,1,512,512]{3,2,1,0:T(8,128)(2,1)} %param.14, f32[2,512,512]{2,1,0:T(8,128)S(1)} %bitcast.79), kind=kOutput, calls=%fused_computation.14 | convolution fusion | flops 1075838976 | bytes 6291464 | tf_op jit(solution)/shard_map/cij,cjk->cik/dot_general | solution.py:60
  197.0 2.7 fusion.3
  199.6 0.1 select_reduce_fusion.4
  199.7 7.2 %all-reduce.2 = (f32[7]{0:T(128)S(1)}, f32[7]{0:T(128)S(1)}) all-reduce(f32[7]{0:T(128)S(1)} %get-tuple-element.25, f32[7]{0:T(128)S(1)} %get-tuple-element.24), channel_id=1, replica_groups=mesh['dp_0'=4,'dp_1'=2,'dp_2'=2,'shard_0'=4,'shard_1'=2] {'dp_0'}, use_global_device_ids=true, to_apply=%region_14.15 | all-reduce | flops 14 | bytes 112 | tf_op jit(solution)/shard_map/psum | solution.py:17
  206.9 3.8 %all-reduce.5 = (f32[7]{0:T(128)S(1)}, f32[7]{0:T(128)S(1)}) all-reduce(f32[7]{0:T(128)S(1)} %get-tuple-element.28, f32[7]{0:T(128)S(1)} %get-tuple-element.29), channel_id=1, replica_groups=mesh['dp_0'=4,'dp_1'=2,'dp_2'=2,'shard_0'=4,'shard_1'=2] {'dp_1'}, use_global_device_ids=true, to_apply=%region_15.16 | all-reduce | flops 14 | bytes 112 | tf_op jit(solution)/shard_map/psum | solution.py:17
  210.7 6.2 %all-reduce.4 = (f32[7]{0:T(128)S(1)}, f32[7]{0:T(128)S(1)}) all-reduce(f32[7]{0:T(128)S(1)} %get-tuple-element.34, f32[7]{0:T(128)S(1)} %get-tuple-element.35), channel_id=1, replica_groups=mesh['dp_0'=4,'dp_1'=2,'dp_2'=2,'shard_0'=4,'shard_1'=2] {'dp_2'}, use_global_device_ids=true, to_apply=%region_16.17 | all-reduce | flops 14 | bytes 112 | tf_op jit(solution)/shard_map/psum | solution.py:17
  216.9 8.7 %all-reduce.1 = (f32[7]{0:T(128)S(1)}, f32[7]{0:T(128)S(1)}) all-reduce(f32[7]{0:T(128)S(1)} %get-tuple-element.32, f32[7]{0:T(128)S(1)} %get-tuple-element.33), channel_id=1, replica_groups=mesh['dp_0'=4,'dp_1'=2,'dp_2'=2,'shard_0'=4,'shard_1'=2] {'shard_0'}, use_global_device_ids=true, to_apply=%region_17.18 | all-reduce | flops 14 | bytes 112 | tf_op jit(solution)/shard_map/psum | solution.py:17
  225.6 5.3 %all-reduce.3 = (f32[7]{0:T(128)S(1)}, f32[7]{0:T(128)S(1)}) all-reduce(f32[7]{0:T(128)S(1)} %get-tuple-element.26, f32[7]{0:T(128)S(1)} %get-tuple-element.27), channel_id=1, replica_groups=mesh['dp_0'=4,'dp_1'=2,'dp_2'=2,'shard_0'=4,'shard_1'=2] {'shard_1'}, use_global_device_ids=true, to_apply=%region_18.19 | all-reduce | flops 14 | bytes 112 | tf_op jit(solution)/shard_map/psum | solution.py:17
  230.9 0.2 select_reduce_fusion.2
  231.1 1.9 multiply_convert_fusion
  233.0 2.0 copy.69
  235.0 7.0 %all-to-all-start.1 = ((bf16[2,512,512]{2,0,1:T(2,128)(2,1)}), bf16[2,512,512]{2,0,1:T(2,128)(2,1)S(1)}, u32[]{:S(2)}, u32[]{:S(2)}) async-start(bf16[2,512,512]{2,0,1:T(2,128)(2,1)} %copy.69), calls=%async_computation.2 | async-start | bytes 2097152 | tf_op jit(solution)/shard_map/all_to_all | solution.py:77
  242.0 0.2 all-gather.2.cloned.1.call-start
  242.2 15.5 %all-to-all-done.1 = bf16[2,512,512]{2,0,1:T(2,128)(2,1)S(1)} async-done(((bf16[2,512,512]{2,0,1:T(2,128)(2,1)}), bf16[2,512,512]{2,0,1:T(2,128)(2,1)S(1)}, u32[]{:S(2)}, u32[]{:S(2)}) %all-to-all-start.1) | async-done | bytes 1048608 | tf_op jit(solution)/shard_map/all_to_all | solution.py:77
  257.7 0.2 copy.70
  257.9 0.1 copy.71
  258.0 0.6 gather_fusion.1
  258.6 0.8 broadcast_select_fusion.1
  259.4 0.0 all-gather.2.cloned.1.call-update
  259.4 0.0 copy-start.4
  259.4 6.1 %fusion = f32[2,1,512,512]{3,2,1,0:T(8,128)} fusion(f32[2,1,512,512]{3,2,1,0:T(8,128)} %param.12, f32[2,512,512]{2,1,0:T(8,128)S(1)} %bitcast.80), kind=kOutput, calls=%fused_computation.6 | convolution fusion | flops 3222798336 | bytes 6291456 | tf_op jit(solution)/shard_map/cji,cjk->cik/dot_general | solution.py:49
  265.6 5.0 %fusion.1 = f32[2,1,512,512]{3,2,1,0:T(8,128)} fusion(f32[2,1,512,512]{3,2,1,0:T(8,128)S(1)} %copy-done.4, f32[2,512,512]{2,1,0:T(8,128)S(1)} %bitcast.81), kind=kOutput, calls=%fused_computation.9 | convolution fusion | flops 3222798336 | bytes 6291456 | tf_op jit(solution)/shard_map/cij,ckj->cik/dot_general | solution.py:48
  270.6 26.5 %all-gather.2.cloned.1.call-done = bf16[11,512,512]{2,1,0:T(8,128)(2,1)} async-done(((bf16[11,32,512]{2,1,0:T(8,128)(2,1)}), bf16[11,512,512]{2,1,0:T(8,128)(2,1)}) %all-gather.2.cloned.1.call-update) | async-done | bytes 5767184 | tf_op jit(solution)/shard_map/all_gather | solution.py:79
  297.1 5.6 %copy.85 = bf16[11,512,512]{2,1,0:T(8,128)(2,1)} copy(bf16[11,512,512]{2,1,0:T(8,128)(2,1)} %all-gather.2.cloned.1.call-done) | data formatting | bytes 11534336
  (17 shorter events, 0.1 us)
Async XLA Ops:
  7.2 185.8 %copy-start = (bf16[2,1,512,512]{3,2,1,0:T(8,128)(2,1)S(1)}, bf16[2,1,512,512]{3,2,1,0:T(8,128)(2,1)}, u32[]{:S(2)}) copy-start(bf16[2,1,512,512]{3,2,1,0:T(8,128)(2,1)} %param.15) | copy-start | bytes 3145732
  7.2 140.0 %reduce-scatter.2.cloned.1.call-start = ((), (), s32[]{:S(2)}) async-start(), calls=%async_computation.3 | async-start | bytes 12255232 | tf_op jit(solution)/shard_map/reduce_scatter | solution.py:39
  15.9 0.7 copy-start.6
  153.5 5.9 %copy-start.5 = (s32[88]{0:T(128)S(1)}, s32[88]{0:T(128)}, u32[]{:S(2)}) copy-start(s32[88]{0:T(128)} %param.10) | copy-start | bytes 1060
  153.5 32.9 %all-to-all-start = ((f32[16,2,32,512]{3,2,1,0:T(8,128)}), f32[16,2,32,512]{3,2,1,0:T(8,128)S(1)}, u32[]{:S(2)}, u32[]{:S(2)}) async-start(f32[16,2,32,512]{3,2,1,0:T(8,128)} %broadcast_select_fusion), calls=%async_computation.1 | async-start | bytes 4194304 | tf_op jit(solution)/shard_map/all_to_all | solution.py:46
  186.4 1.3 copy-start.2
  187.9 2.2 copy-start.3
  235.0 22.7 %all-to-all-start.1 = ((bf16[2,512,512]{2,0,1:T(2,128)(2,1)}), bf16[2,512,512]{2,0,1:T(2,128)(2,1)S(1)}, u32[]{:S(2)}, u32[]{:S(2)}) async-start(bf16[2,512,512]{2,0,1:T(2,128)(2,1)} %copy.69), calls=%async_computation.2 | async-start | bytes 2097152 | tf_op jit(solution)/shard_map/all_to_all | solution.py:77
  242.0 55.1 %all-gather.2.cloned.1.call-start = ((), (), s32[]{:S(2)}) async-start(), calls=%async_computation.4 | async-start | bytes 6127616 | tf_op jit(solution)/shard_map/all_gather | solution.py:79
  259.4 6.2 %copy-start.4 = (f32[2,1,512,512]{3,2,1,0:T(8,128)S(1)}, f32[2,1,512,512]{3,2,1,0:T(8,128)}, u32[]{:S(2)}) copy-start(f32[2,1,512,512]{3,2,1,0:T(8,128)} %param.11) | copy-start | bytes 6291460
  297.1 5.6 %copy-start.1 = (bf16[2,1,512,512]{3,2,1,0:T(8,128)(2,1)S(1)}, bf16[2,1,512,512]{3,2,1,0:T(8,128)(2,1)}, u32[]{:S(2)}) copy-start(bf16[2,1,512,512]{3,2,1,0:T(8,128)(2,1)} %param.15) | copy-start | bytes 3145732
Sparse Core Ops, SparseCore 0:
  16.0 131.0 reduce-scatter.1
  259.6 37.5 all-gather.1
where the time goes:
time: 310 us
  waiting for transfers between devices  199 us (64%)
  blocking collectives  31.1 us (10%)
  other arithmetic  21.1 us (7%)
  local copies, waits for them, and re-layouts  16 us (5%)
  matrix products  15.1 us (5%)
  between operations  14.2 us (5%)
  starting transfers between devices  13.1 us (4%)
    reduce_scatter x1, waiting for transfers between devices, on_device(): row_share = lax.psum_scatter(partials, DP, scatter_dimension=1, tiled=True)  130 us
    psum x5, blocking collectives, by_axis(): x = lax.psum(x, axis)  31.1 us
    all_to_all x1, waiting for transfers between devices, on_device(): lax.all_to_all(outgoing, DP, split_axis=0, concat_axis=2, tiled=True)  26.7 us
    all_gather x1, waiting for transfers between devices, on_device(): update = lax.all_gather(pieces, DP, axis=1, tiled=True)  26.5 us
    all_to_all x1, waiting for transfers between devices, on_device(): lax.all_to_all(slot_update, DP, split_axis=1, concat_axis=0, tiled=True)  15.5 us
    convert_element_type x1, other arithmetic, on_device(): partials = gradients[0].astype(jnp.float32)  8.67 us
    unnamed x15, local copies, waits for them, and re-layouts  7.59 us
    all_to_all x1, starting transfers between devices, on_device(): lax.all_to_all(slot_update, DP, split_axis=1, concat_axis=0, tiled=True)  6.96 us
  transfers between devices with their start and end apart: 4, of which 4 were waited for; matrix products, arithmetic and copies ran while one was open for 4% of the time, Pallas kernels for 0%

commit v1 on v0

--- a/solution.py
+++ b/solution.py
@@ -43,7 +43,9 @@
     outgoing = jnp.take(share_padded, source, axis=0).reshape(
         replicas, capacity, block_width // replicas, block_width
     )
-    arrived = lax.all_to_all(outgoing, DP, split_axis=0, concat_axis=2, tiled=True)
+    arrived = jnp.concatenate(
+        lax.all_to_all(jnp.stack(jnp.split(outgoing, lax.axis_size(DP), axis=0)), DP, 0, 0), axis=2
+    )
     summed = arrived[0]
     left_gram = jnp.einsum("cij,ckj->cik", summed, summed, precision=lax.Precision.HIGHEST)
     right_gram = jnp.einsum("cji,cjk->cik", summed, summed, precision=lax.Precision.HIGHEST)

time: 310 us -> 319 us (1.029)
  local copies, waits for them, and re-layouts: 16 us -> 26.5 us
    unnamed x15 -> x30, local copies, waits for them, and re-layouts: 7.59 us -> 17.5 us
where the time goes in v1:
time: 319 us
  waiting for transfers between devices  199 us (62%)
  blocking collectives  31.1 us (10%)
  local copies, waits for them, and re-layouts  26.5 us (8%)
  other arithmetic  19.8 us (6%)
  matrix products  15.1 us (5%)
  between operations  14.2 us (4%)
  starting transfers between devices  13.1 us (4%)
    reduce_scatter x1, waiting for transfers between devices, on_device(): row_share = lax.psum_scatter(partials, DP, scatter_dimension=1, tiled=True)  130 us
    psum x5, blocking collectives, by_axis(): x = lax.psum(x, axis)  31.1 us
    all_to_all x1, waiting for transfers between devices, on_device(): lax.all_to_all(jnp.stack(jnp.split(outgoing, lax.axis_size(DP), axis=0)),...  26.7 us
    all_gather x1, waiting for transfers between devices, on_device(): update = lax.all_gather(pieces, DP, axis=1, tiled=True)  26.5 us
    unnamed x30, local copies, waits for them, and re-layouts  17.5 us
    all_to_all x1, waiting for transfers between devices, on_device(): lax.all_to_all(slot_update, DP, split_axis=1, concat_axis=0, tiled=True)  15.5 us
    convert_element_type x1, other arithmetic, on_device(): partials = gradients[0].astype(jnp.float32)  8.67 us
    all_to_all x1, starting transfers between devices, on_device(): lax.all_to_all(slot_update, DP, split_axis=1, concat_axis=0, tiled=True)  6.96 us
  transfers between devices with their start and end apart: 4, of which 4 were waited for; matrix products, arithmetic and copies ran while one was open for 4% of the time, Pallas kernels for 0%

profile of v1, /device:TPU:1, one launch (start us, length us, event | category | flops | bytes accessed | tf_op | source)
XLA Modules:
  0.0 318.9 jit_solution(14419111593601905721)
XLA Ops:
  7.2 8.7 %bitcast_convert_fusion = f32[11,512,512]{2,1,0:T(8,128)} fusion(bf16[1,11,512,512]{3,2,1,0:T(8,128)(2,1)} %param.8), kind=kLoop, calls=%fused_computation.2 | loop fusion | flops 2883584 | bytes 17301504 | tf_op jit(solution)/shard_map/convert_element_type | solution.py:38
  15.9 0.6 copy-done.6
  16.9 130.3 %reduce-scatter.2.cloned.1.call-done = f32[11,32,512]{2,1,0:T(8,128)} async-done(((f32[11,512,512]{2,1,0:T(8,128)}), f32[11,32,512]{2,1,0:T(8,128)}) %reduce-scatter.2.cloned.1.call-update) | async-done | bytes 720912 | tf_op jit(solution)/shard_map/reduce_scatter | solution.py:39
  147.2 1.2 concatenate.3
  148.4 2.0 gather_fusion
  150.4 1.8 broadcast_select_fusion
  152.2 0.7 fusion.25
  152.8 0.7 fusion.24
  153.5 0.7 fusion.23
  154.2 0.7 fusion.22
  154.8 0.7 fusion.21
  155.5 0.7 fusion.20
  156.1 0.7 fusion.19
  156.8 0.7 fusion.18
  157.5 0.7 fusion.17
  158.1 0.7 fusion.16
  158.8 0.7 fusion.15
  159.5 0.7 fusion.14
  160.1 0.7 fusion.13
  160.8 0.7 fusion.12
  161.5 0.7 fusion.11
  162.1 0.7 fusion.10
  162.8 5.9 %all-to-all-start = ((f32[16,1,2,32,512]{4,3,2,1,0:T(8,128)}), f32[16,1,2,32,512]{4,3,2,1,0:T(8,128)S(1)}, u32[]{:S(2)}, u32[]{:S(2)}) async-start(f32[16,1,2,32,512]{4,3,2,1,0:T(8,128)} %fusion.10), calls=%async_computation.1 | async-start | bytes 4194304 | tf_op jit(solution)/shard_map/all_to_all | solution.py:47
  169.0 26.7 %all-to-all-done = f32[16,1,2,32,512]{4,3,2,1,0:T(8,128)S(1)} async-done(((f32[16,1,2,32,512]{4,3,2,1,0:T(8,128)}), f32[16,1,2,32,512]{4,3,2,1,0:T(8,128)S(1)}, u32[]{:S(2)}, u32[]{:S(2)}) %all-to-all-start) | async-done | bytes 2097184 | tf_op jit(solution)/shard_map/all_to_all | solution.py:47
  195.7 0.3 multiply_multiply_fusion
  196.0 1.1 copy-done.2
  197.0 0.2 copy.67
  197.3 2.0 copy.63
  199.2 0.3 copy-done.3
  199.5 2.8 sqrt_add_fusion
  202.3 4.0 %multiply_reduce_fusion = (f32[2]{0:T(128)S(1)}, f32[2,512,512]{2,1,0:T(8,128)}) fusion(bf16[2,1,512,512]{3,2,1,0:T(8,128)(2,1)S(1)} %copy-done, bf16[2,1,512,512]{3,2,1,0:T(8,128)(2,1)} %param.14, f32[2,512,512]{2,1,0:T(8,128)S(1)} %bitcast.140), kind=kOutput, calls=%fused_computation.14 | convolution fusion | flops 1075838976 | bytes 6291464 | tf_op jit(solution)/shard_map/cij,cjk->cik/dot_general | solution.py:62
  206.3 2.7 fusion.3
  209.0 7.2 %all-reduce.2 = (f32[7]{0:T(128)S(1)}, f32[7]{0:T(128)S(1)}) all-reduce(f32[7]{0:T(128)S(1)} %get-tuple-element.25, f32[7]{0:T(128)S(1)} %get-tuple-element.24), channel_id=1, replica_groups=mesh['dp_0'=4,'dp_1'=2,'dp_2'=2,'shard_0'=4,'shard_1'=2] {'dp_0'}, use_global_device_ids=true, to_apply=%region_14.15 | all-reduce | flops 14 | bytes 112 | tf_op jit(solution)/shard_map/psum | solution.py:17
  216.2 3.8 %all-reduce.5 = (f32[7]{0:T(128)S(1)}, f32[7]{0:T(128)S(1)}) all-reduce(f32[7]{0:T(128)S(1)} %get-tuple-element.28, f32[7]{0:T(128)S(1)} %get-tuple-element.29), channel_id=1, replica_groups=mesh['dp_0'=4,'dp_1'=2,'dp_2'=2,'shard_0'=4,'shard_1'=2] {'dp_1'}, use_global_device_ids=true, to_apply=%region_15.16 | all-reduce | flops 14 | bytes 112 | tf_op jit(solution)/shard_map/psum | solution.py:17
  220.0 6.2 %all-reduce.4 = (f32[7]{0:T(128)S(1)}, f32[7]{0:T(128)S(1)}) all-reduce(f32[7]{0:T(128)S(1)} %get-tuple-element.34, f32[7]{0:T(128)S(1)} %get-tuple-element.35), channel_id=1, replica_groups=mesh['dp_0'=4,'dp_1'=2,'dp_2'=2,'shard_0'=4,'shard_1'=2] {'dp_2'}, use_global_device_ids=true, to_apply=%region_16.17 | all-reduce | flops 14 | bytes 112 | tf_op jit(solution)/shard_map/psum | solution.py:17
  226.2 8.7 %all-reduce.1 = (f32[7]{0:T(128)S(1)}, f32[7]{0:T(128)S(1)}) all-reduce(f32[7]{0:T(128)S(1)} %get-tuple-element.32, f32[7]{0:T(128)S(1)} %get-tuple-element.33), channel_id=1, replica_groups=mesh['dp_0'=4,'dp_1'=2,'dp_2'=2,'shard_0'=4,'shard_1'=2] {'shard_0'}, use_global_device_ids=true, to_apply=%region_17.18 | all-reduce | flops 14 | bytes 112 | tf_op jit(solution)/shard_map/psum | solution.py:17
  234.9 5.3 %all-reduce.3 = (f32[7]{0:T(128)S(1)}, f32[7]{0:T(128)S(1)}) all-reduce(f32[7]{0:T(128)S(1)} %get-tuple-element.26, f32[7]{0:T(128)S(1)} %get-tuple-element.27), channel_id=1, replica_groups=mesh['dp_0'=4,'dp_1'=2,'dp_2'=2,'shard_0'=4,'shard_1'=2] {'shard_1'}, use_global_device_ids=true, to_apply=%region_18.19 | all-reduce | flops 14 | bytes 112 | tf_op jit(solution)/shard_map/psum | solution.py:17
  240.4 1.9 multiply_convert_fusion
  242.3 2.0 copy.71
  244.3 7.0 %all-to-all-start.1 = ((bf16[2,512,512]{2,0,1:T(2,128)(2,1)}), bf16[2,512,512]{2,0,1:T(2,128)(2,1)S(1)}, u32[]{:S(2)}, u32[]{:S(2)}) async-start(bf16[2,512,512]{2,0,1:T(2,128)(2,1)} %copy.71), calls=%async_computation.2 | async-start | bytes 2097152 | tf_op jit(solution)/shard_map/all_to_all | solution.py:79
  251.3 0.2 all-gather.2.cloned.1.call-start
  251.6 15.5 %all-to-all-done.1 = bf16[2,512,512]{2,0,1:T(2,128)(2,1)S(1)} async-done(((bf16[2,512,512]{2,0,1:T(2,128)(2,1)}), bf16[2,512,512]{2,0,1:T(2,128)(2,1)S(1)}, u32[]{:S(2)}, u32[]{:S(2)}) %all-to-all-start.1) | async-done | bytes 1048608 | tf_op jit(solution)/shard_map/all_to_all | solution.py:79
  267.3 0.6 gather_fusion.1
  267.9 0.8 broadcast_select_fusion.1
  268.8 6.1 %fusion = f32[2,1,512,512]{3,2,1,0:T(8,128)} fusion(f32[2,1,512,512]{3,2,1,0:T(8,128)} %param.12, f32[2,512,512]{2,1,0:T(8,128)S(1)} %bitcast.141), kind=kOutput, calls=%fused_computation.6 | convolution fusion | flops 3222798336 | bytes 6291456 | tf_op jit(solution)/shard_map/cji,cjk->cik/dot_general | solution.py:51
  274.9 5.0 %fusion.1 = f32[2,1,512,512]{3,2,1,0:T(8,128)} fusion(f32[2,1,512,512]{3,2,1,0:T(8,128)S(1)} %copy-done.4, f32[2,512,512]{2,1,0:T(8,128)S(1)} %bitcast.142), kind=kOutput, calls=%fused_computation.9 | convolution fusion | flops 3222798336 | bytes 6291456 | tf_op jit(solution)/shard_map/cij,ckj->cik/dot_general | solution.py:50
  279.9 26.5 %all-gather.2.cloned.1.call-done = bf16[11,512,512]{2,1,0:T(8,128)(2,1)} async-done(((bf16[11,32,512]{2,1,0:T(8,128)(2,1)}), bf16[11,512,512]{2,1,0:T(8,128)(2,1)}) %all-gather.2.cloned.1.call-update) | async-done | bytes 5767184 | tf_op jit(solution)/shard_map/all_gather | solution.py:81
  306.4 5.6 %copy.102 = bf16[11,512,512]{2,1,0:T(8,128)(2,1)} copy(bf16[11,512,512]{2,1,0:T(8,128)(2,1)} %all-gather.2.cloned.1.call-done) | data formatting | bytes 11534336
  (32 shorter events, 1.3 us)
Async XLA Ops:
  7.2 195.1 %copy-start = (bf16[2,1,512,512]{3,2,1,0:T(8,128)(2,1)S(1)}, bf16[2,1,512,512]{3,2,1,0:T(8,128)(2,1)}, u32[]{:S(2)}) copy-start(bf16[2,1,512,512]{3,2,1,0:T(8,128)(2,1)} %param.15) | copy-start | bytes 3145732
  7.2 140.0 %reduce-scatter.2.cloned.1.call-start = ((), (), s32[]{:S(2)}) async-start(), calls=%async_computation.3 | async-start | bytes 12255232 | tf_op jit(solution)/shard_map/reduce_scatter | solution.py:39
  15.9 0.7 copy-start.6
  162.8 5.9 %copy-start.5 = (s32[88]{0:T(128)S(1)}, s32[88]{0:T(128)}, u32[]{:S(2)}) copy-start(s32[88]{0:T(128)} %param.10) | copy-start | bytes 1060
  162.8 32.9 %all-to-all-start = ((f32[16,1,2,32,512]{4,3,2,1,0:T(8,128)}), f32[16,1,2,32,512]{4,3,2,1,0:T(8,128)S(1)}, u32[]{:S(2)}, u32[]{:S(2)}) async-start(f32[16,1,2,32,512]{4,3,2,1,0:T(8,128)} %fusion.10), calls=%async_computation.1 | async-start | bytes 4194304 | tf_op jit(solution)/shard_map/all_to_all | solution.py:47
  195.7 1.3 copy-start.2
  197.3 2.2 copy-start.3
  244.3 22.7 %all-to-all-start.1 = ((bf16[2,512,512]{2,0,1:T(2,128)(2,1)}), bf16[2,512,512]{2,0,1:T(2,128)(2,1)S(1)}, u32[]{:S(2)}, u32[]{:S(2)}) async-start(bf16[2,512,512]{2,0,1:T(2,128)(2,1)} %copy.71), calls=%async_computation.2 | async-start | bytes 2097152 | tf_op jit(solution)/shard_map/all_to_all | solution.py:79
  251.3 55.1 %all-gather.2.cloned.1.call-start = ((), (), s32[]{:S(2)}) async-start(), calls=%async_computation.4 | async-start | bytes 6127616 | tf_op jit(solution)/shard_map/all_gather | solution.py:81
  268.7 6.2 %copy-start.4 = (f32[2,1,512,512]{3,2,1,0:T(8,128)S(1)}, f32[2,1,512,512]{3,2,1,0:T(8,128)}, u32[]{:S(2)}) copy-start(f32[2,1,512,512]{3,2,1,0:T(8,128)} %param.11) | copy-start | bytes 6291460
  306.4 5.6 %copy-start.1 = (bf16[2,1,512,512]{3,2,1,0:T(8,128)(2,1)S(1)}, bf16[2,1,512,512]{3,2,1,0:T(8,128)(2,1)}, u32[]{:S(2)}) copy-start(bf16[2,1,512,512]{3,2,1,0:T(8,128)(2,1)} %param.15) | copy-start | bytes 3145732
Sparse Core Ops, SparseCore 0:
  16.0 131.0 reduce-scatter.1
  268.9 37.5 all-gather.1
